TPU v7x, 512 devices: a whole 4x8x8 slice. The times are simulated.
512 devices in a mesh: dp: 8 (over y_hi, core), ep: 64 (over x, y_lo, z).
Axes of the slice: x: 4, y: 8 (y_hi: 4, y_lo: 2; y = y_hi * 2 + y_lo), z: 8, core: 2. Of those that a mesh axis runs over, the one named last changes fastest.
Arguments:
- hidden_in: bfloat16 [12288, 4096], P(('dp', 'ep')), may hold values from -6 to 6
- expert_ids: int32 [12288, 2], P(('dp', 'ep')), may hold values from 0 to 63, all different within a row; in each aligned block of 24 rows (0 to 23, 24 to 47, ...) at most 2 rows name the same one
- route_logits: float32 [12288, 64], P(('dp', 'ep')), may hold values from -10 to 10
- first_weight: bfloat16 [64, 4096, 1024], P('ep', None, 'dp'), may hold values from -0.09375 to 0.09375
- second_weight: bfloat16 [64, 1024, 4096], P('ep', None, 'dp'), may hold values from -0.1875 to 0.1875
- queries: bfloat16 [12288, 2048], P(('dp', 'ep')), may hold values from -140 to 140
- span_keys: bfloat16 [12288, 2048], P(('dp', 'ep')), may hold values from -7 to 7
- span_values: bfloat16 [12288, 2048], P(('dp', 'ep')), may hold values from -6 to 6
- cache_keys: bfloat16 [512, 72, 2048], P(('dp', 'ep')), may hold values from -6 to 6
- cache_values: bfloat16 [512, 72, 2048], P(('dp', 'ep')), may hold values from -6 to 6
- valid_frames: int32 [512], P(('dp', 'ep')), may hold values from 1 to 3
Outputs:
- mixed: bfloat16 [12288, 4096], P(('dp', 'ep'))
- attended: bfloat16 [12288, 2048], P(('dp', 'ep'))
Inputs may be any that keep to these rules, and one draw needn't show every extreme that they name: `expert_ids`: each token names two different experts. In the rows of one device (24 rows) no expert is named more than 2 times, a bound that some block reaches.
All inputs are finite; a program needn't handle non-finite values.
Results may differ from a plain program's by a relative error of at most 0.0057.
Values may be sent and summed in bfloat16 or wider, within the bound.
A program may use at most 128 MiB of HBM per device.

v0:
```python
import math

import jax
import jax.numpy as jnp
from jax import lax
from jax.sharding import PartitionSpec as P

HEADS = 16
HEAD_DIM = 128
FRAME_TOK = 24


def activate(pre):
    return jax.nn.gelu(pre, approximate=True).astype(jnp.bfloat16)


def expert_slots(expert_ids):
    flat_ids = expert_ids.reshape(-1)
    assigned = flat_ids.shape[0]
    row_ids = lax.broadcasted_iota(jnp.int32, (assigned, assigned), 0)
    col_ids = lax.broadcasted_iota(jnp.int32, (assigned, assigned), 1)
    same_expert = (flat_ids[:, None] == flat_ids[None, :]) & (col_ids < row_ids)
    return jnp.sum(same_expert.astype(jnp.int32), axis=1).reshape(expert_ids.shape)


def attend(queries, span_keys, span_values, cache_keys, cache_values, valid_count):
    token_count = queries.shape[0]
    cache_len = cache_keys.shape[0]
    key_rows = jnp.concatenate([cache_keys, span_keys], axis=0)
    value_rows = jnp.concatenate([cache_values, span_values], axis=0)
    query_heads = queries.reshape(token_count, HEADS, HEAD_DIM)
    key_heads = key_rows.reshape(-1, HEADS, HEAD_DIM)
    value_heads = value_rows.reshape(-1, HEADS, HEAD_DIM)
    scores = jnp.einsum(
        "thd,khd->htk", query_heads, key_heads, preferred_element_type=jnp.float32
    ) * (1.0 / math.sqrt(HEAD_DIM))
    position = lax.broadcasted_iota(jnp.int32, (key_rows.shape[0],), 0)
    usable = (position >= cache_len) | (position // FRAME_TOK < valid_count)
    scores = jnp.where(usable[None, None, :], scores, -1e30)
    row_max = jnp.max(scores, axis=2, keepdims=True)
    weights = jnp.exp(scores - row_max)
    weights = (weights / jnp.sum(weights, axis=2, keepdims=True)).astype(jnp.bfloat16)
    result = jnp.einsum("htk,khd->thd", weights, value_heads, preferred_element_type=jnp.float32)
    return result.astype(jnp.bfloat16).reshape(token_count, HEADS * HEAD_DIM)


def shards(
    hidden_in,
    expert_ids,
    route_logits,
    first_weight,
    second_weight,
    queries,
    span_keys,
    span_values,
    cache_keys,
    cache_values,
    valid_frames,
):
    tokens, model_width = hidden_in.shape
    experts = lax.axis_size("ep")
    capacity = max(2, 8 * tokens // (3 * experts))
    slots = expert_slots(expert_ids)
    places = expert_ids * capacity + slots
    place_ids = lax.broadcasted_iota(jnp.int32, (tokens, experts * capacity), 1)
    picks = [places[:, column : column + 1] == place_ids for column in range(2)]
    chooser = (picks[0] | picks[1]).astype(jnp.bfloat16)
    dispatch = lax.dot_general(
        chooser, hidden_in, (((0,), (0,)), ((), ())), preferred_element_type=jnp.float32
    )
    dispatch = dispatch.astype(jnp.bfloat16).reshape(experts, capacity, model_width)
    expert_cols = lax.broadcasted_iota(jnp.int32, route_logits.shape, 1)
    chosen = jnp.stack(
        [
            jnp.sum(
                jnp.where(expert_cols == expert_ids[:, column : column + 1], route_logits, 0.0),
                axis=1,
            )
            for column in range(2)
        ],
        axis=1,
    )
    gates = jax.nn.softmax(chosen, axis=1)
    first_local = first_weight[0]
    second_local = second_weight[0]
    received = lax.all_to_all(dispatch, "ep", split_axis=0, concat_axis=0, tiled=True)
    sources, item_count, _ = received.shape
    expert_rows = received.reshape(sources * item_count, model_width)
    hidden = activate(
        jnp.dot(
            expert_rows,
            lax.all_gather(first_local, "dp", axis=1, tiled=True),
            preferred_element_type=jnp.float32,
        )
    )
    result = jnp.dot(
        hidden,
        lax.all_gather(second_local, "dp", axis=1, tiled=True),
        preferred_element_type=jnp.float32,
    ).astype(jnp.bfloat16)
    outputs = result.reshape(sources, item_count, model_width)
    returned = lax.all_to_all(outputs, "ep", split_axis=0, concat_axis=0, tiled=True)
    attended = attend(
        queries, span_keys, span_values, cache_keys[0], cache_values[0], valid_frames[0]
    )
    flat_back = returned.reshape(experts * capacity, model_width)
    running = jnp.zeros((tokens, model_width), jnp.float32)
    for column in range(2):
        picked = jnp.dot(
            picks[column].astype(jnp.bfloat16), flat_back, preferred_element_type=jnp.float32
        )
        running = running + gates[:, column : column + 1] * picked
    mixed = running.astype(jnp.bfloat16)
    return (mixed, attended)


def solution(mesh):
    placed = (
        P(("dp", "ep"), None),
        P(("dp", "ep"), None),
        P(("dp", "ep"), None),
        P("ep", None, "dp"),
        P("ep", None, "dp"),
        P(("dp", "ep"), None),
        P(("dp", "ep"), None),
        P(("dp", "ep"), None),
        P(("dp", "ep"), None, None),
        P(("dp", "ep"), None, None),
        P(("dp", "ep")),
    )
    return jax.shard_map(
        shards,
        mesh=mesh,
        in_specs=placed,
        out_specs=(P(("dp", "ep"), None), P(("dp", "ep"), None)),
        check_vma=False,
    )
```

profile of v0, /device:TPU:1, one launch (start us, length us, event | category | flops | bytes accessed | tf_op | source)
XLA Modules:
  0.0 263.4 jit_solution(3099905430017032602)
XLA Ops:
  7.2 0.7 all-gather.7.cloned.1.call-update
  8.0 0.7 all-gather.5.cloned.1.call-update
  8.7 0.8 copy.35
  9.4 0.1 eq.61
  9.5 0.2 convert_reduce_fusion
  9.7 0.1 reshape.64
  9.9 0.7 multiply_add_fusion
  10.6 0.5 convolution_convert_fusion
  11.1 0.7 reshape.65
  11.9 47.1 %all_to_all.10 = bf16[64,2,4096]{2,1,0:T(2,128)(2,1)S(1)} all-to-all(bf16[64,2,4096]{2,1,0:T(2,128)(2,1)S(1)} %reshape.65), channel_id=1, replica_groups=mesh['dp'=8,'ep'=64] {'ep'}, dimensions={0} | all-to-all | bytes 2097152 | tf_op jit(solution)/shard_map/all_to_all | solution.py:86
  59.0 0.4 reshape.66
  59.5 52.2 %all-gather.7.cloned.1.call-done = bf16[1,1024,4096]{2,1,0:T(8,128)(2,1)} async-done(((bf16[1,1024,512]{2,1,0:T(8,128)(2,1)}), bf16[1,1024,4096]{2,1,0:T(8,128)(2,1)}) %all-gather.7.cloned.1.call-update) | async-done | bytes 8388624 | tf_op jit(solution)/shard_map/all_gather | solution.py:98
  111.6 94.6 %all-gather.5.cloned.1.call-done = bf16[1,4096,1024]{2,1,0:T(8,128)(2,1)} async-done(((bf16[1,4096,128]{2,1,0:T(8,128)(2,1)}), bf16[1,4096,1024]{2,1,0:T(8,128)(2,1)}) %all-gather.5.cloned.1.call-update) | async-done | bytes 8388624 | tf_op jit(solution)/shard_map/all_gather | solution.py:92
  206.2 8.3 %fusion.5 = bf16[128,4096]{1,0:T(8,128)(2,1)S(1)} fusion(bf16[1,1024,4096]{2,1,0:T(8,128)(2,1)} %all-gather.7.cloned.1.call-done, bf16[128,4096]{1,0:T(8,128)(2,1)S(1)} %reshape.66, bf16[1,4096,1024]{2,1,0:T(8,128)(2,1)} %all-gather.5.cloned.1.call-done), kind=kOutput, calls=%fused_computation.5 | convolution fusion | flops 2149187584 | bytes 18874368 | tf_op jit(solution)/shard_map/dot_general | solution.py:96
  214.6 1.5 reshape.67
  216.1 11.2 %all-to-all-start.1 = ((bf16[64,2,4096]{2,1,0:T(2,128)(2,1)}), bf16[64,2,4096]{2,1,0:T(2,128)(2,1)S(1)}, u32[]{:S(2)}, u32[]{:S(2)}) async-start(bf16[64,2,4096]{2,1,0:T(2,128)(2,1)} %reshape.67), calls=%async_computation.1 | async-start | bytes 2097152 | tf_op jit(solution)/shard_map/all_to_all | solution.py:102
  228.3 0.5 fusion.70
  228.8 0.3 fusion.14
  229.1 0.7 copy.62
  229.8 0.2 select_reduce_fusion
  230.0 24.8 %all-to-all-done.1 = bf16[64,2,4096]{2,1,0:T(2,128)(2,1)S(1)} async-done(((bf16[64,2,4096]{2,1,0:T(2,128)(2,1)}), bf16[64,2,4096]{2,1,0:T(2,128)(2,1)S(1)}, u32[]{:S(2)}, u32[]{:S(2)}) %all-to-all-start.1) | async-done | bytes 1048608 | tf_op jit(solution)/shard_map/all_to_all | solution.py:102
  254.8 0.4 reshape.68
  255.3 0.3 convolution_multiply_fusion.1
  255.6 1.0 fusion.9
  (32 shorter events, 0.6 us)
Async XLA Ops:
  7.2 3.4 %copy-start = (bf16[24,4096]{1,0:T(8,128)(2,1)S(1)}, bf16[24,4096]{1,0:T(8,128)(2,1)}, u32[]{:S(2)}) copy-start(bf16[24,4096]{1,0:T(8,128)(2,1)} %param.11) | copy-start | bytes 589828
  7.2 104.5 %all-gather.7.cloned.1.call-start = ((), (), s32[]{:S(2)}) async-start(), calls=%async_computation.3 | async-start | bytes 9437184 | tf_op jit(solution)/shard_map/all_gather | solution.py:98
  7.9 198.3 %all-gather.5.cloned.1.call-start = ((), (), s32[]{:S(2)}) async-start(), calls=%async_computation.2 | async-start | bytes 9437184 | tf_op jit(solution)/shard_map/all_gather | solution.py:92
  59.4 167.9 %copy-start.1 = (bf16[1,72,2048]{2,1,0:T(8,128)(2,1)S(1)}, bf16[1,72,2048]{2,1,0:T(8,128)(2,1)}, u32[]{:S(2)}) copy-start(bf16[1,72,2048]{2,1,0:T(8,128)(2,1)} %param.20) | copy-start | bytes 884740
  59.4 168.0 %copy-start.2 = (bf16[1,72,2048]{2,1,0:T(8,128)(2,1)S(1)}, bf16[1,72,2048]{2,1,0:T(8,128)(2,1)}, u32[]{:S(2)}) copy-start(bf16[1,72,2048]{2,1,0:T(8,128)(2,1)} %param.19) | copy-start | bytes 884740
  59.4 168.8 %copy-start.3 = (bf16[24,2048]{1,0:T(8,128)(2,1)S(1)}, bf16[24,2048]{1,0:T(8,128)(2,1)}, u32[]{:S(2)}) copy-start(bf16[24,2048]{1,0:T(8,128)(2,1)} %param.18) | copy-start | bytes 294916
  59.4 168.8 %copy-start.4 = (bf16[24,2048]{1,0:T(8,128)(2,1)S(1)}, bf16[24,2048]{1,0:T(8,128)(2,1)}, u32[]{:S(2)}) copy-start(bf16[24,2048]{1,0:T(8,128)(2,1)} %param.17) | copy-start | bytes 294916
  59.5 168.9 %copy-start.7 = (bf16[24,2048]{1,0:T(8,128)(2,1)S(1)}, bf16[24,2048]{1,0:T(8,128)(2,1)}, u32[]{:S(2)}) copy-start(bf16[24,2048]{1,0:T(8,128)(2,1)} %param.16) | copy-start | bytes 294916
  214.5 15.2 %copy-start.6 = (s32[24,2]{0,1:T(2,128)S(1)}, s32[24,2]{0,1:T(2,128)}, u32[]{:S(2)}) copy-start(s32[24,2]{0,1:T(2,128)} %param.12) | copy-start | bytes 580
  214.6 15.2 %copy-start.5 = (f32[24,64]{1,0:T(8,128)S(1)}, f32[24,64]{1,0:T(8,128)}, u32[]{:S(2)}) copy-start(f32[24,64]{1,0:T(8,128)} %param.13) | copy-start | bytes 18436
  216.1 38.8 %all-to-all-start.1 = ((bf16[64,2,4096]{2,1,0:T(2,128)(2,1)}), bf16[64,2,4096]{2,1,0:T(2,128)(2,1)S(1)}, u32[]{:S(2)}, u32[]{:S(2)}) async-start(bf16[64,2,4096]{2,1,0:T(2,128)(2,1)} %reshape.67), calls=%async_computation.1 | async-start | bytes 2097152 | tf_op jit(solution)/shard_map/all_to_all | solution.py:102
Sparse Core Ops, SparseCore 0:
  10.1 101.4 all-gather.6
  113.7 92.4 all-gather.4
where the time goes:
time: 264 us; the launch traced here: 263 us
  waiting for transfers between devices  173 us (66%)
  blocking collectives  47.1 us (18%)
  between operations  14.9 us (6%)
  starting transfers between devices  11.3 us (4%)
  matrix products  10.9 us (4%)
  local copies, waits for them, and re-layouts  5.08 us (2%)
    all_gather x1, waiting for transfers between devices, shards(): lax.all_gather(first_local, 'dp', axis=1, tiled=True)  94.6 us
    all_gather x1, waiting for transfers between devices, shards(): lax.all_gather(second_local, 'dp', axis=1, tiled=True)  52.2 us
    all_to_all x1, blocking collectives, shards(): lax.all_to_all(dispatch, 'ep', split_axis=0, concat_axis=0, tiled=True)  47.1 us
    all_to_all x1, waiting for transfers between devices, shards(): lax.all_to_all(outputs, 'ep', split_axis=0, concat_axis=0, tiled=True)  24.8 us
    all_to_all x1, starting transfers between devices, shards(): lax.all_to_all(outputs, 'ep', split_axis=0, concat_axis=0, tiled=True)  11.2 us
    dot_general x1, matrix products, shards(): jnp.dot(hidden, lax.all_gather(second_local, 'dp', axis=1, tiled=True), p...  8.33 us
  transfers between devices with their start and end apart: 3, of which 3 were waited for; matrix products, arithmetic and copies ran while one was open for 2% of the time, Pallas kernels for 0%

commit v1 on v0

v1 whole, which is shorter than its diff:
```python
import functools
import math

import jax
import jax.numpy as jnp
from jax import lax
from jax.experimental import pallas as pl
from jax.experimental.pallas import tpu as pltpu
from jax.sharding import PartitionSpec as P

HEAD_DIM = 128
FRAME_TOK = 24
MESH = pl.DeviceIdType.MESH
F32, BF16, I32 = jnp.float32, jnp.bfloat16, jnp.int32
NQ = 4
NC = 2
NZ = 8
PAD = 32


def iota(shape, axis):
    return lax.broadcasted_iota(I32, shape, axis)


def kernel(
    hid, ids, logits, w1, w2, qr, sk, sv, ck, cv, vf,
    mixed, attended,
    tok, disp, rows, w1all, w2all, act, out, ret, meta, mix_send, mix_recv, aperm,
    z_send, z_recv, u_send, u_recv, w_send, w_recv, s_send, s_recv, a_send, a_recv,
    r_send, r_recv, m_send, m_recv, x_send, x_recv,
):
    tokens, width = hid.shape
    hidden_cols = w1.shape[1]
    out_cols = w2.shape[1]
    half = width // 2
    ep = lax.axis_index("ep")
    dp = lax.axis_index("dp")
    peers = lax.axis_size("ep")
    nu = peers // NZ
    u, z = ep // NZ, lax.rem(ep, NZ)
    q, c = dp // NC, lax.rem(dp, NC)
    zp, zm = lax.rem(z + 1, NZ), lax.rem(z + NZ - 1, NZ)
    qp, qm, qo = lax.rem(q + 1, NQ), lax.rem(q + 3, NQ), lax.rem(q + 2, NQ)
    at_zp, at_zm = {"ep": u * NZ + zp}, {"ep": u * NZ + zm}
    at_qp, at_qm, at_qo = {"dp": qp * NC + c}, {"dp": qm * NC + c}, {"dp": qo * NC + c}
    sibling = {"dp": q * NC + (1 - c)}

    def remote(src, dst, send, recv, to):
        return pltpu.make_async_remote_copy(
            src_ref=src, dst_ref=dst, send_sem=send, recv_sem=recv, device_id=to, device_id_type=MESH
        )

    barrier = pltpu.get_barrier_semaphore()
    for to in (at_qp, at_qm, at_qo, sibling):
        pl.semaphore_signal(barrier, inc=1, device_id=to, device_id_type=MESH)

    def greet(i, carry):
        pl.semaphore_signal(
            barrier, inc=1, device_id={"ep": lax.rem(ep + i, peers)}, device_id_type=MESH
        )
        return carry

    lax.fori_loop(1, peers, greet, 0)

    ids_f = ids[...].astype(F32)
    first, second = ids_f[:, 0:1], ids_f[:, 1:2]
    wide = NZ * PAD
    lane, sub = iota((tokens, wide), 1), iota((tokens, wide), 0)
    first_row = jnp.sum(jnp.where(lane == sub, first, 0.0), axis=0, keepdims=True)
    second_row = jnp.sum(jnp.where(lane == sub, second, 0.0), axis=0, keepdims=True)
    ahead = (sub < lane) & (lane < tokens)

    def row_places(row):
        same = (first == row).astype(F32) + (second == row).astype(F32)
        slot = jnp.sum(jnp.where(ahead, same, 0.0), axis=0, keepdims=True)
        lanes = iota((1, wide), 1)
        return jnp.where(lanes < tokens, row * 2.0 + slot + 1.0, 0.0)

    def col_places(col):
        same = (col == first_row).astype(F32) + (col == second_row).astype(F32)
        slot = jnp.sum(jnp.where(lane < sub, same, 0.0), axis=1, keepdims=True)
        return col * 2.0 + slot

    place_rows = (row_places(first_row), row_places(second_row))
    place_cols = (col_places(first), col_places(second))
    expert_lane = iota(logits.shape, 1).astype(F32)
    chosen = [
        jnp.sum(jnp.where(expert_lane == col, logits[...], 0.0), axis=1, keepdims=True)
        for col in (first, second)
    ]
    top = jnp.maximum(chosen[0], chosen[1])
    weight = [jnp.exp(x - top) for x in chosen]
    total = weight[0] + weight[1]
    gates = [x / total for x in weight]
    lanes = iota((tokens, 128), 1)
    record = jnp.zeros((tokens, 128), F32)
    for k, value in enumerate((*place_cols, *gates)):
        record = jnp.where(lanes == k, value, record)
    meta[q] = record
    tok[0, 0:tokens, :] = hid[...]
    tail_rows = PAD - tokens
    tail_sub = iota((tail_rows, wide), 0)
    tail = jnp.where(tail_sub == 0, place_rows[0], jnp.where(tail_sub == 1, place_rows[1], 0.0))
    tok[0, tokens:PAD, :] = jnp.zeros((tail_rows, width), BF16)
    tok[0, tokens:PAD, 0:wide] = tail.astype(BF16)

    pl.semaphore_wait(barrier, NQ + peers - 1)

    tops, bottoms = pl.ds(0, half), pl.ds(half, half)
    mine = q * NC + c

    def w1_copy(src, shard, part, sems, number, to):
        return remote(src, w1all.at[shard, part], sems[0].at[number], sems[1].at[number], to)

    w_sems = (w_send, w_recv)
    from_m, from_p, from_o = qm * NC + c, qp * NC + c, qo * NC + c
    w_copies = [
        w1_copy(w1.at[tops], mine, tops, w_sems, 0, at_qp),
        w1_copy(w1.at[bottoms], mine, bottoms, w_sems, 1, at_qm),
        w1_copy(w1.at[bottoms], mine, bottoms, w_sems, 2, at_qp),
        w1_copy(w1.at[tops], mine, tops, w_sems, 3, at_qm),
    ]
    for copy in w_copies:
        copy.start()

    def z_copy(src, dst, number, to, part=None):
        a, b = (tok.at[src], tok.at[dst]) if part is None else (tok.at[src, part], tok.at[dst, part])
        return remote(a, b, z_send.at[number], z_recv.at[number], to)

    low, high = pl.ds(0, PAD // 2), pl.ds(PAD // 2, PAD // 2)
    down = [z_copy(0, 1, 0, at_zm), z_copy(1, 2, 1, at_zm), z_copy(2, 3, 2, at_zm), z_copy(3, 4, 3, at_zm, low)]
    up = [z_copy(0, 7, 4, at_zp), z_copy(7, 6, 5, at_zp), z_copy(6, 5, 6, at_zp), z_copy(5, 4, 7, at_zp, high)]
    down[0].start()
    up[0].start()

    s_sems = (s_send, s_recv)
    other = q * NC + (1 - c)
    s_copies = [
        remote(w2, w2all.at[c], s_send.at[8], s_recv.at[8], sibling),
        w1_copy(w1.at[tops], mine, tops, s_sems, 0, sibling),
        w1_copy(w1.at[bottoms], mine, bottoms, s_sems, 1, sibling),
    ]
    for copy in s_copies:
        copy.start()
    m_copies = [
        remote(meta.at[q], meta.at[q], m_send.at[i], m_recv.at[i], to)
        for i, to in enumerate((at_qp, at_qm, at_qo))
    ]
    for copy in m_copies:
        copy.start()
    w1all[mine] = w1[...]
    w2all[c] = w2[...]

    cache_len = ck.shape[0]
    frame = iota((tokens, cache_len), 1)
    usable = frame < vf[0] * FRAME_TOK
    scale = 1.0 / math.sqrt(HEAD_DIM)
    heads = qr.shape[1] // HEAD_DIM

    def head(h, carry):
        cols = pl.ds(pl.multiple_of(h * HEAD_DIM, HEAD_DIM), HEAD_DIM)
        query = qr[:, cols]
        contract = (((1,), (1,)), ((), ()))
        old = lax.dot_general(query, ck[:, cols], contract, preferred_element_type=F32) * scale
        new = lax.dot_general(query, sk[:, cols], contract, preferred_element_type=F32) * scale
        old = jnp.where(usable, old, -1e30)
        peak = jnp.maximum(jnp.max(old, axis=1, keepdims=True), jnp.max(new, axis=1, keepdims=True))
        old, new = jnp.exp(old - peak), jnp.exp(new - peak)
        norm = jnp.sum(old, axis=1, keepdims=True) + jnp.sum(new, axis=1, keepdims=True)
        old, new = (old / norm).astype(BF16), (new / norm).astype(BF16)
        result = jnp.dot(old, cv[:, cols], preferred_element_type=F32)
        result += jnp.dot(new, sv[:, cols], preferred_element_type=F32)
        attended[:, cols] = result.astype(BF16)
        return carry

    per_step = heads // 4
    for step in range(4):
        lax.fori_loop(step * per_step, (step + 1) * per_step, head, 0)
        down[step].wait_recv()
        up[step].wait_recv()
        if step < 3:
            down[step + 1].start()
            up[step + 1].start()

    lanes = iota((1, wide), 1)
    place = [jnp.zeros((1, wide), F32), jnp.zeros((1, wide), F32)]
    for r in range(NZ):
        block = tok[r, tokens:PAD, 0:wide].astype(F32)
        if r:
            block = pltpu.roll(block, r * PAD, 1)
        for k in range(2):
            place[k] = place[k] + block[k : k + 1, :]
    picks_rows = nu * NZ * 2
    row, lane = iota((picks_rows, wide), 0), iota((picks_rows, wide), 1)
    wanted = ((row // (NZ * 2)) * NZ + z) * 2 + row % 2 + 1
    wanted_f = wanted.astype(F32)
    hit = (place[0] == wanted_f) | (place[1] == wanted_f)
    hit = hit & (lane // PAD == (row % (NZ * 2)) // 2)
    chooser = jnp.where(hit, 1.0, 0.0).astype(BF16)
    step_cols = min(512, width)

    def select(i, carry):
        cols = pl.ds(pl.multiple_of(i * step_cols, step_cols), step_cols)
        block = tok[:, :, cols].reshape(wide, step_cols)
        picked = jnp.dot(chooser, block, preferred_element_type=F32)
        disp[:, :, cols] = picked.astype(BF16).reshape(nu, NZ * 2, step_cols)
        return carry

    lax.fori_loop(0, width // step_cols, select, 0)

    def u_copy(i):
        to = lax.rem(u + i, nu)
        return remote(disp.at[to], rows.at[u], u_send, u_recv, {"ep": to * NZ + z})

    def start_u(i, carry):
        u_copy(i).start()
        return carry

    lax.fori_loop(1, nu, start_u, 0)
    rows[u] = disp[u]

    def w_recv_at(shard, part, number):
        return w1_copy(w1all.at[shard, part], shard, part, w_sems, number, at_qp)

    w_forward = [
        w1_copy(w1all.at[from_m, tops], from_m, tops, w_sems, 4, at_qp),
        w1_copy(w1all.at[from_p, bottoms], from_p, bottoms, w_sems, 5, at_qm),
    ]

    def to_sibling(shard, part, number):
        copy = w1_copy(w1all.at[shard, part], shard, part, s_sems, number, sibling)
        copy.start()
        s_copies.append(copy)

    w_recv_at(from_m, tops, 0).wait_recv()
    w_forward[0].start()
    to_sibling(from_m, tops, 2)
    w_recv_at(from_p, bottoms, 1).wait_recv()
    w_forward[1].start()
    to_sibling(from_p, bottoms, 3)
    w_recv_at(from_m, bottoms, 2).wait_recv()
    to_sibling(from_m, bottoms, 4)
    w_recv_at(from_p, tops, 3).wait_recv()
    to_sibling(from_p, tops, 5)

    if nu > 1:
        remote(
            disp.at[pl.ds(0, nu - 1)], rows.at[pl.ds(0, nu - 1)], u_send, u_recv, sibling
        ).wait_recv()

    def sibling_arrived(shard, part, number):
        w1_copy(w1all.at[shard, part], shard, part, s_sems, number, sibling).wait_recv()

    sib_m, sib_p, sib_o = qm * NC + 1 - c, qp * NC + 1 - c, qo * NC + 1 - c
    sibling_arrived(other, tops, 0)
    sibling_arrived(other, bottoms, 1)
    sibling_arrived(sib_m, tops, 2)
    sibling_arrived(sib_p, bottoms, 3)
    sibling_arrived(sib_m, bottoms, 4)
    sibling_arrived(sib_p, tops, 5)

    expert_rows = picks_rows

    def first_matmul(i, carry):
        ahead_by = i // NC
        ahead_by = jnp.where(ahead_by == 2, 3, jnp.where(ahead_by == 3, 2, ahead_by))
        shard = lax.rem(q + ahead_by, NQ) * NC + lax.rem(i, NC)
        pre = jnp.dot(rows[...].reshape(expert_rows, width), w1all[shard], preferred_element_type=F32)
        cols = pl.ds(pl.multiple_of(shard * hidden_cols, 128), hidden_cols)
        act[0, :, cols] = jax.nn.gelu(pre, approximate=True).astype(BF16)
        return carry

    lax.fori_loop(0, 6, first_matmul, 0)
    w_recv_at(from_o, tops, 4).wait_recv()
    to_sibling(from_o, tops, 6)
    w_recv_at(from_o, bottoms, 5).wait_recv()
    to_sibling(from_o, bottoms, 7)
    sibling_arrived(sib_o, tops, 6)
    sibling_arrived(sib_o, bottoms, 7)
    lax.fori_loop(6, 8, first_matmul, 0)

    act_half = expert_rows // 2
    tops, bottoms = pl.ds(0, act_half), pl.ds(act_half, act_half)

    def a_copy(src, dst, part, number, to):
        return remote(act.at[src, part], act.at[dst, part], a_send.at[number], a_recv.at[number], to)

    a_copies = [
        a_copy(0, 3, tops, 0, at_qp),
        a_copy(0, 1, bottoms, 1, at_qm),
        a_copy(0, 3, bottoms, 2, at_qp),
        a_copy(0, 1, tops, 3, at_qm),
        a_copy(3, 2, tops, 4, at_qp),
        a_copy(1, 2, bottoms, 5, at_qm),
    ]
    for copy in a_copies[:4]:
        copy.start()
    a_copies[0].wait_recv()
    a_copies[4].start()
    a_copies[1].wait_recv()
    a_copies[5].start()
    for copy in a_copies[2:]:
        copy.wait_recv()
    remote(w2, w2all.at[1 - c], s_send.at[8], s_recv.at[8], sibling).wait_recv()

    blocks = 4
    chunk = NQ * expert_rows // blocks
    all_hidden = act.shape[2]

    def second_matmul(i, carry):
        row = iota((chunk, NQ * expert_rows), 0) + i * chunk
        col = iota((chunk, NQ * expert_rows), 1)
        inner = col % expert_rows
        owner = (q + col // expert_rows) % NQ
        hit = (row // 8 == inner // 2) & ((row % 8) // 2 == owner) & (row % 2 == inner % 2)
        order = jnp.where(hit, 1.0, 0.0).astype(BF16)
        source = act[...].reshape(NQ * expert_rows, all_hidden)
        aperm[...] = jnp.dot(order, source, preferred_element_type=F32).astype(BF16)
        dests = pl.ds(i * (chunk // 8), chunk // 8)
        for part in range(NC):
            result = jnp.dot(aperm[...], w2all[part], preferred_element_type=F32)
            result = result.reshape(chunk // 8, 8, out_cols).astype(BF16)
            out[dests, :, part * out_cols : (part + 1) * out_cols] = result
        return carry

    lax.fori_loop(0, blocks, second_matmul, 0)

    def r_copy(i):
        to_u, r = lax.rem(u + i // NZ, nu), lax.rem(i, NZ)
        to = to_u * NZ + lax.rem(z + r, NZ)
        return remote(out.at[to_u * NZ + r], ret.at[ep], r_send, r_recv, {"ep": to})

    def start_r(i, carry):
        r_copy(i).start()
        return carry

    lax.fori_loop(1, peers, start_r, 0)
    ret[ep] = out[u * NZ]
    for copy in m_copies:
        copy.wait_recv()
    remote(
        out.at[pl.ds(0, peers - 1)], ret.at[pl.ds(0, peers - 1)], r_send, r_recv, sibling
    ).wait_recv()

    info = meta[...].reshape(NQ * tokens, 128)
    row, lane = iota((NQ * tokens, peers * 8), 0), iota((NQ * tokens, peers * 8), 1)
    held = (lane // 8) * 2 + lane % 2
    own = (lane % 8) // 2 == row // tokens
    held_f = held.astype(F32)
    mix_cols = NC * out_cols
    returned = ret[...].astype(F32).reshape(peers * 8, mix_cols).astype(BF16)
    running = jnp.zeros((NQ * tokens, mix_cols), F32)
    for k in range(2):
        hit = own & (info[:, k : k + 1] == held_f)
        pick = jnp.where(hit, 1.0, 0.0).astype(BF16)
        picked = jnp.dot(pick, returned, preferred_element_type=F32)
        running = running + info[:, 2 + k : 3 + k] * picked
    for i in range(NQ):
        mix_send[i] = running[i * tokens : (i + 1) * tokens].astype(BF16)
    x_copies = [
        remote(mix_send.at[to], mix_recv.at[q], x_send.at[i], x_recv.at[i], at)
        for i, (to, at) in enumerate(((qp, at_qp), (qm, at_qm), (qo, at_qo)))
    ]
    for copy in x_copies:
        copy.start()

    def place_cols_of(chip, block):
        mixed[:, pl.ds(pl.multiple_of(chip * mix_cols, 128), mix_cols)] = block

    place_cols_of(q, mix_send[q])
    for copy in (*w_copies, *w_forward, *down, *up, *s_copies, *m_copies, *a_copies):
        copy.wait_send()
    if nu > 1:
        remote(
            disp.at[pl.ds(0, nu - 1)], rows.at[pl.ds(0, nu - 1)], u_send, u_recv, sibling
        ).wait_send()
    remote(
        out.at[pl.ds(0, peers - 1)], ret.at[pl.ds(0, peers - 1)], r_send, r_recv, sibling
    ).wait_send()
    for copy, chip in zip(x_copies, (qm, qp, qo)):
        copy.wait_recv()
        place_cols_of(chip, mix_recv[chip])
    for copy in x_copies:
        copy.wait_send()


def shards(
    hidden_in, expert_ids, route_logits, first_weight, second_weight,
    queries, span_keys, span_values, cache_keys, cache_values, valid_frames,
):
    tokens, width = hidden_in.shape
    peers = lax.axis_size("ep")
    nu = peers // NZ
    _, _, hidden_cols = first_weight.shape
    _, all_hidden, out_cols = second_weight.shape
    mix_cols = NC * out_cols
    expert_rows = peers * 2
    vmem = pl.BlockSpec(memory_space=pltpu.VMEM)
    dma = pltpu.SemaphoreType.DMA
    return pl.pallas_call(
        kernel,
        out_shape=(
            jax.ShapeDtypeStruct((tokens, width), BF16),
            jax.ShapeDtypeStruct(queries.shape, BF16),
        ),
        in_specs=[vmem] * 10 + [pl.BlockSpec(memory_space=pltpu.SMEM)],
        out_specs=(vmem, vmem),
        scratch_shapes=[
            pltpu.VMEM((NZ, PAD, width), BF16),
            pltpu.VMEM((nu, NZ * 2, width), BF16),
            pltpu.VMEM((nu, NZ * 2, width), BF16),
            pltpu.VMEM((NQ * NC, width, hidden_cols), BF16),
            pltpu.VMEM((NC, all_hidden, out_cols), BF16),
            pltpu.VMEM((NQ, expert_rows, all_hidden), BF16),
            pltpu.VMEM((peers, 8, mix_cols), BF16),
            pltpu.VMEM((peers, 8, mix_cols), BF16),
            pltpu.VMEM((NQ, tokens, 128), F32),
            pltpu.VMEM((NQ, tokens, mix_cols), BF16),
            pltpu.VMEM((NQ, tokens, mix_cols), BF16),
            pltpu.VMEM((expert_rows, all_hidden), BF16),
            dma((8,)), dma((8,)),
            dma, dma,
            dma((6,)), dma((6,)),
            dma((9,)), dma((9,)),
            dma((6,)), dma((6,)),
            dma, dma,
            dma((3,)), dma((3,)),
            dma((3,)), dma((3,)),
        ],
        compiler_params=pltpu.CompilerParams(
            collective_id=0, has_side_effects=True, vmem_limit_bytes=60 * 1024 * 1024
        ),
    )(
        hidden_in, expert_ids, route_logits, first_weight[0], second_weight[0],
        queries, span_keys, span_values, cache_keys[0], cache_values[0], valid_frames,
    )


def solution(mesh):
    placed = (
        P(("dp", "ep"), None),
        P(("dp", "ep"), None),
        P(("dp", "ep"), None),
        P("ep", None, "dp"),
        P("ep", None, "dp"),
        P(("dp", "ep"), None),
        P(("dp", "ep"), None),
        P(("dp", "ep"), None),
        P(("dp", "ep"), None, None),
        P(("dp", "ep"), None, None),
        P(("dp", "ep")),
    )
    return jax.shard_map(
        shards,
        mesh=mesh,
        in_specs=placed,
        out_specs=(P(("dp", "ep"), None), P(("dp", "ep"), None)),
        check_vma=False,
    )
```

time: 264 us -> 163 us (0.62)
  waiting for transfers between devices: 173 us -> 0 us
  Pallas kernels: 0 us -> 156 us
  blocking collectives: 47.1 us -> 0 us
  between operations: 14.9 us -> 1.3 us
  starting transfers between devices: 11.3 us -> 0 us
  matrix products: 10.9 us -> 0 us
    pallas_call x0 -> x1, Pallas kernels: none -> 156 us  [shards(): pl.pallas_call(kernel, out_shape=(jax.ShapeDtypeStruct((tokens, width), B...]
    all_gather x2 -> x0, waiting for transfers between devices: 147 us -> none  [the longest x1 94.6 us: shards(): lax.all_gather(first_local, 'dp', axis=1, tiled=True)]
    all_to_all x1 -> x0, blocking collectives: 47.1 us -> none  [shards(): lax.all_to_all(dispatch, 'ep', split_axis=0, concat_axis=0, tiled=True)]
    all_to_all x1 -> x0, waiting for transfers between devices: 24.8 us -> none  [shards(): lax.all_to_all(outputs, 'ep', split_axis=0, concat_axis=0, tiled=True)]
    all_to_all x1 -> x0, starting transfers between devices: 11.2 us -> none  [shards(): lax.all_to_all(outputs, 'ep', split_axis=0, concat_axis=0, tiled=True)]
    dot_general x5 -> x0, matrix products: 10.5 us -> none  [the longest x1 8.33 us: shards(): jnp.dot(hidden, lax.all_gather(second_local, 'dp', axis=1, tiled=True), p...]
    reshape x7 -> x0, local copies, waits for them, and re-layouts: 3.87 us -> none  [the longest x1 1.49 us: shards(): outputs = result.reshape(sources, item_count, model_width)]
    unnamed x19 -> x7, local copies, waits for them, and re-layouts: 0.9 us -> 3.65 us
  transfers between devices with their start and end apart: 3 -> 0, of which waited for: 3 -> 0; matrix products, arithmetic and copies ran while one was open for 2% -> 0% of each run, Pallas kernels for 0% -> 0%
where the time goes in v1:
time: 163 us; the launch traced here: 161 us
  Pallas kernels  156 us (96%)
  local copies, waits for them, and re-layouts  3.65 us (2%)
    pallas_call x1, Pallas kernels, shards(): pl.pallas_call(kernel, out_shape=(jax.ShapeDtypeStruct((tokens, width), B...  156 us
    unnamed x7, local copies, waits for them, and re-layouts  3.65 us

profile of v1, /device:TPU:1, one launch (start us, length us, event | category | flops | bytes accessed | tf_op | source)
XLA Modules:
  0.0 160.6 jit_solution(4091811667948862688)
XLA Ops:
  1.3 0.0 copy-start.1
  1.3 0.7 copy-done.1
  2.0 0.7 copy.13.ids
  2.6 155.6 %shard_map.122 = (bf16[24,4096]{1,0:T(8,128)(2,1)}, bf16[24,2048]{1,0:T(8,128)(2,1)}) custom-call(bf16[24,4096]{1,0:T(8,128)(2,1)} %hid.1, s32[24,2]{1,0:T(8,128)} %copy.13.ids, f32[24,64]{1,0:T(8,128)} %logits.1, bf16[4096,128]{1,0:T(8,128)(2,1)} %bitcast.4, bf16[1024,512]{1,0:T(8,128)(2,1)} %bitcast.5, bf16[24,2048]{1,0:T(8,128)(2,1)} %qr.1, ...), custom_call_target="tpu_custom_call" | custom-call | tf_op jit(solution)/shard_map/pallas_call | solution.py:400
  158.3 0.0 copy-start
  158.3 1.6 %copy.17 = bf16[24,4096]{1,0:T(8,128)(2,1)} copy(bf16[24,4096]{1,0:T(8,128)(2,1)} %get-tuple-element.4) | data formatting | bytes 393216
  159.9 0.0 copy-done
  159.9 0.6 copy.18
Async XLA Ops:
  1.3 0.7 copy-start.1
  158.3 1.7 %copy-start = (bf16[24,2048]{1,0:T(8,128)(2,1)S(1)}, bf16[24,2048]{1,0:T(8,128)(2,1)}, u32[]{:S(2)}) copy-start(bf16[24,2048]{1,0:T(8,128)(2,1)} %get-tuple-element.5) | copy-start | bytes 294916
